TPU v7x, 512 devices: a whole 4x8x8 slice. The times are simulated.
512 devices in a mesh: fsdp: 64 (over y, x, core), model: 8 (over z).
Axes of the slice: x: 4, y: 8, z: 8, core: 2. Of those that a mesh axis runs over, the one named last changes fastest.
Arguments:
- train_query: float32 [2560, 4096], P('fsdp', 'model'), may hold values from -0.3125 to 0.3125
- drift_query: float32 [2560, 4096], P('fsdp', 'model'), may hold values from -6 to 6
- spread_query: float32 [2560, 4096], P('fsdp', 'model'), may hold values from 0.1 to 10
- train_key: float32 [2560, 1024], P('fsdp', 'model'), may hold values from -0.3125 to 0.3125
- drift_key: float32 [2560, 1024], P('fsdp', 'model'), may hold values from -6 to 6
- spread_key: float32 [2560, 1024], P('fsdp', 'model'), may hold values from 0.1 to 10
- train_value: float32 [2560, 1024], P('fsdp', 'model'), may hold values from -0.3125 to 0.3125
- drift_value: float32 [2560, 1024], P('fsdp', 'model'), may hold values from -6 to 6
- spread_value: float32 [2560, 1024], P('fsdp', 'model'), may hold values from 0.1 to 10
- norm_train: float32 [2560], P(('fsdp', 'model')), may hold values from 0.25 to 1.75
- norm_step: float32 [2560], P(('fsdp', 'model')), may hold values from -0.3 to 0.3
Outputs:
- serve_query: bfloat16 [2560, 4096], P(None, 'model')
- serve_key: bfloat16 [2560, 1024], P(None, 'model')
- serve_value: bfloat16 [2560, 1024], P(None, 'model')
- factor_query: float32 [4096], P('model')
- factor_key: float32 [1024], P('model')
- factor_value: float32 [1024], P('model')
- serve_norm: bfloat16 [2560], replicated
- fresh_query: float32 [2560, 4096], P('fsdp', 'model')
- fresh_key: float32 [2560, 1024], P('fsdp', 'model')
- fresh_value: float32 [2560, 1024], P('fsdp', 'model')
All inputs are finite; a program needn't handle non-finite values. Where the computation divides by a largest or mean magnitude, that divisor is 1e-20 or more.
Results may differ from a plain program's by a relative error of at most 0.001.
Values may be sent and summed in bfloat16 or wider, within the bound.
No kernel may reach another device: no remote copies, remote signals or barrier semaphores. Data moves between devices by JAX's collectives and lax.ppermute only.
A program may use at most 64 MiB of HBM per device.

v0:
```python
import functools

import jax
import jax.numpy as jnp
from jax import lax
from jax.experimental import pallas as pl
from jax.experimental.pallas import tpu as pltpu
from jax.sharding import Mesh
from jax.sharding import PartitionSpec as P


Y, X, C, Z = "fsdp_0", "fsdp_1", "fsdp_2", "model"
FSDP = (Y, X, C)
NY, NX = 8, 4

learn_rate = 0.02
decay_rate = 0.05
tiny_value = 1e-08

LANES = 128
SPAN = 125.0
FLOOR = 1e-28
PARTS = 2


def padded(rows):
    return -(-rows // 8) * 8


def spot():
    return tuple(lax.axis_index(a) for a in (Y, X, C))


def encode_kernel(widths, norm_train, norm_step, *refs):
    n = len(widths)
    sources, fresh_refs, wire = refs[: 3 * n], refs[3 * n : 4 * n], refs[4 * n]
    ins, sems = refs[4 * n + 1 : -1], refs[-1]
    loads = [pltpu.make_async_copy(s, d, sems.at[i]) for i, (s, d) in enumerate(zip(sources, ins))]
    for load in loads:
        load.start()
    copies = wire.shape[0]
    rows = ins[0].shape[0]
    slabs = sum(w // LANES for w in widths)
    slab = 0
    for at, width in enumerate(widths):
        train, drift, spread = ins[3 * at : 3 * at + 3]
        for load in loads[3 * at : 3 * at + 3]:
            load.wait()
        for k in range(width // LANES):
            cols = slice(k * LANES, (k + 1) * LANES)
            t = train[:, cols]
            fresh = t - learn_rate * (
                drift[:, cols] / (jnp.sqrt(spread[:, cols]) + tiny_value) + decay_rate * t
            )
            fresh_refs[at][:, cols] = fresh
            left = jnp.maximum(jnp.max(jnp.abs(fresh), axis=0, keepdims=True), FLOOR)
            parts = []
            scale = jnp.zeros_like(left)
            for _ in range(PARTS):
                parts.append(left.astype(jnp.bfloat16))
                part = parts[-1].astype(jnp.float32)
                scale, left = scale + part, left - part
            code = jnp.exp2(fresh * (SPAN / scale)).astype(jnp.bfloat16)
            for c in range(copies):
                wire[c, slab * rows : (slab + 1) * rows, :] = code
                for p, part in enumerate(parts):
                    row = slabs * rows + p * slabs + slab
                    wire[c, row : row + 1, :] = part
            slab += 1
    used = slabs * (rows + PARTS)
    few = norm_train.shape[0]
    y, x, c = spot()
    start = (place(y, x, c) * lax.axis_size(Z) + lax.axis_index(Z)) * few
    lane = lax.broadcasted_iota(jnp.int32, (1, LANES), 1) - lax.rem(start, LANES)
    lane = jnp.where(lane < 0, lane + LANES, lane)
    gain = jnp.zeros((1, LANES), jnp.float32)
    for i in range(few):
        gain = jnp.where(lane == i, norm_train[i] + norm_step[i], gain)
    gain = gain.astype(jnp.bfloat16)
    for copy in range(copies):
        wire[copy, used : used + 1, :] = gain


def encode(copies, norms, arrays):
    rows = arrays[0].shape[0]
    widths = tuple(a.shape[1] for a in arrays[::3])
    slabs = sum(w // LANES for w in widths)
    out = [pltpu.VMEM(a.shape, a.dtype) for a in arrays[::3]]
    out.append(pltpu.VMEM((copies, padded(slabs * (rows + PARTS) + 1), LANES), jnp.bfloat16))
    vmem = pl.BlockSpec(memory_space=pltpu.VMEM)
    return pl.pallas_call(
        functools.partial(encode_kernel, widths),
        out_shape=out,
        in_specs=[pl.BlockSpec(memory_space=pltpu.SMEM)] * 2
        + [pl.BlockSpec(memory_space=pltpu.HBM)] * len(arrays),
        out_specs=[vmem] * len(out),
        scratch_shapes=[pltpu.VMEM(a.shape, a.dtype) for a in arrays]
        + [pltpu.SemaphoreType.DMA((len(arrays),))],
        compiler_params=pltpu.CompilerParams(vmem_limit_bytes=16 * 2**20),
        name="encode",
    )(*(in_hbm(a) for a in norms), *(in_hbm(a) for a in arrays))


def prepare_kernel(row, own, out):
    rows = own[:, row - row % 8 : row - row % 8 + 8, :].astype(jnp.float32)[:, row % 8, :]
    rows = rows.astype(out.dtype)
    for i in range(out.shape[0]):
        out[i] = rows


def prepare(row, copies, own):
    vmem = pl.BlockSpec(memory_space=pltpu.VMEM)
    return pl.pallas_call(
        functools.partial(prepare_kernel, row),
        out_shape=pltpu.VMEM((copies, own.shape[0], LANES), own.dtype),
        in_specs=[vmem],
        out_specs=vmem,
        compiler_params=pltpu.CompilerParams(vmem_limit_bytes=4 * 2**20),
        name="prepare",
    )(in_vmem(own))


def pack_kernel(*refs):
    for i, ref in enumerate(refs[:-1]):
        refs[-1][i] = ref[...]


def pack(arrays):
    vmem = pl.BlockSpec(memory_space=pltpu.VMEM)
    return pl.pallas_call(
        pack_kernel,
        out_shape=pltpu.VMEM((len(arrays), *arrays[0].shape), arrays[0].dtype),
        in_specs=[vmem] * len(arrays),
        out_specs=vmem,
        compiler_params=pltpu.CompilerParams(vmem_limit_bytes=4 * 2**20),
        name="pack",
    )(*(in_vmem(a) for a in arrays))


def in_hbm(value):
    return pltpu.with_memory_space_constraint(value, pltpu.HBM)


def in_vmem(value):
    return pltpu.with_memory_space_constraint(value, pltpu.VMEM)


def decode_kernel(widths, rows, *refs):
    n = len(widths)
    wires = [refs[i // 4].at[i % 4] for i in range(8)]
    refs = refs[2:]
    serve, factor, scratch = refs[:n], refs[n : 2 * n], refs[2 * n :]
    stage, ratios, sems = scratch[:n], scratch[n], scratch[n + 1]
    slabs = sum(w // LANES for w in widths)
    low = slabs * rows
    y, x, mine = spot()
    kind = lax.rem(x + 2 * y, NX)
    best = None
    for i, wire in enumerate(wires):
        tail = wire[:, low:, :].astype(jnp.float32)
        scale = tail[:, :slabs]
        for p in range(1, PARTS):
            scale = scale + tail[:, p * slabs : (p + 1) * slabs]
        ratios[i] = scale
        top = jnp.max(scale, axis=0)
        best = top if best is None else jnp.maximum(best, top)
    slab = 0
    for at, width in enumerate(widths):
        for k in range(width // LANES):
            factor[at][:, k * LANES : (k + 1) * LANES] = best[slab : slab + 1]
            slab += 1
    share = 1.0 / (SPAN * best)
    for i in range(8):
        ratios[i] = ratios[i] * share

    def copy(at, y):
        return pltpu.make_async_copy(stage[at].at[y], serve[at].at[y], sems.at[at, y])

    def body(y, _):
        for i, wire in enumerate(wires):
            x = lax.rem(kind + i % 4 + 2 * y, NX)
            c = mine if i < 4 else 1 - mine
            slab = 0
            for at, width in enumerate(widths):
                for k in range(width // LANES):
                    cols = slice(k * LANES, (k + 1) * LANES)
                    code = wire[y, slab * rows : (slab + 1) * rows, :].astype(jnp.float32)
                    ratio = ratios[i, y, slab : slab + 1, :]
                    stage[at][y, x, c, :, cols] = (jnp.log2(code) * ratio).astype(jnp.bfloat16)
                    slab += 1
        for at in range(n):
            copy(at, y).start()
        return 0

    lax.fori_loop(0, NY, body, 0)
    for at in range(n):
        for y in range(NY):
            copy(at, y).wait()


def decode(widths, rows, own, other):
    stage = [(NY, NX, 2, rows, w) for w in widths]
    vmem = pl.BlockSpec(memory_space=pltpu.VMEM)
    slabs = sum(w // LANES for w in widths)
    out = [jax.ShapeDtypeStruct(s, jnp.bfloat16) for s in stage]
    out += [jax.ShapeDtypeStruct((1, w), jnp.float32) for w in widths]
    return pl.pallas_call(
        functools.partial(decode_kernel, widths, rows),
        out_shape=out,
        in_specs=[vmem] * 2,
        out_specs=[pl.BlockSpec(memory_space=pl.ANY)] * len(widths) + [vmem] * len(widths),
        scratch_shapes=[pltpu.VMEM(s, jnp.bfloat16) for s in stage]
        + [
            pltpu.VMEM((8, NY, slabs, LANES), jnp.float32),
            pltpu.SemaphoreType.DMA((len(widths), NY)),
        ],
        compiler_params=pltpu.CompilerParams(vmem_limit_bytes=16 * 2**20),
        name="decode",
    )(in_vmem(own), in_vmem(other))


def norm_kernel(gains, _, norm):
    few = norm.shape[0] * LANES // (NY * NX * 2)
    row = lax.broadcasted_iota(jnp.int32, (padded(norm.shape[0]), NY), 0)
    chip = lax.broadcasted_iota(jnp.int32, (padded(norm.shape[0]), NY), 1)
    lane = lax.broadcasted_iota(jnp.int32, (NY, LANES), 1)
    own_y = lax.broadcasted_iota(jnp.int32, (NY, LANES), 0)
    total = jnp.zeros((padded(norm.shape[0]), LANES), jnp.float32)
    for k in range(NX):
        for c in range(2):
            start = lambda y: ((y * NX + lax.rem(k + 2 * y, NX)) * 2 + c) * few
            values = jnp.sum(gains[k, c].astype(jnp.float32), axis=0)
            here = lane >= lax.rem(start(own_y), LANES)
            for j in range(2):
                part = jnp.where(here if j == 0 else ~here, values, 0.0).astype(jnp.bfloat16)
                pick = jnp.where(lax.div(start(chip), LANES) + j == row, 1.0, 0.0)
                total = total + jnp.dot(
                    pick.astype(jnp.bfloat16), part, preferred_element_type=jnp.float32
                )
    norm[...] = total[: norm.shape[0]].astype(norm.dtype)


def gather_norm(few, gains, after):
    return pl.pallas_call(
        norm_kernel,
        out_shape=jax.ShapeDtypeStruct((NY * NX * 2 * few // LANES, LANES), jnp.bfloat16),
        in_specs=[pl.BlockSpec(memory_space=pltpu.VMEM)] * 2,
        out_specs=pl.BlockSpec(memory_space=pltpu.VMEM),
        compiler_params=pltpu.CompilerParams(vmem_limit_bytes=4 * 2**20),
        name="gather_norm",
    )(gains, after)


def place(y, x, c):
    return ((y % NY) * NX + x % NX) * 2 + c


SPOTS = [(y, x, c) for y in range(NY) for x in range(NX) for c in range(2)]


def come_from(value, source):
    return lax.ppermute(value, FSDP, [(place(*source(*s)), place(*s)) for s in SPOTS])


def per_device(n_z, *args):
    arrays, norms = args[:9], args[9:]
    rows = arrays[0].shape[0]
    widths = tuple(a.shape[1] for a in arrays[::3])
    *fresh, wire = encode(NY, norms, arrays)
    same_kind = [[place(y, k - 2 * y, c) for y in range(NY)] for c in range(2) for k in range(NX)]
    own = lax.all_to_all(wire, FSDP, 0, 0, axis_index_groups=same_kind, tiled=True)
    up = come_from(own, lambda y, x, c: (y, x + 1, c))
    down = come_from(own, lambda y, x, c: (y, x - 1, c))
    side = come_from(own, lambda y, x, c: (y + 1 - 2 * c, x, c))
    used = sum(w // LANES for w in widths) * (rows + PARTS)
    gain = prepare(used, NX * 2 * n_z, own)
    rest = [
        [
            (place(y, k - 2 * y, c) * n_z) + z
            for k in range(NX)
            for c in range(2)
            for z in range(n_z)
        ]
        for y in range(NY)
    ]
    gains = lax.all_to_all(gain, FSDP + (Z,), 0, 0, axis_index_groups=rest, tiled=True)
    gains = gains.reshape(NX, 2, n_z, NY, LANES)
    own = pack((own, up, side, down))
    other = come_from(own, lambda y, x, c: (y, x, 1 - c))

    out = decode(widths, rows, own, other)
    norm = gather_norm(norms[0].shape[0] * n_z, gains, out[3])
    serve = [s.reshape(-1, s.shape[-1]) for s in out[:3]]
    factor = [f.reshape(-1) for f in out[3:]]
    return (*serve, *factor, norm.reshape(-1), *fresh)


def solution(mesh):
    split = Mesh(mesh.devices.reshape(NY, NX, 2, mesh.shape["model"]), (Y, X, C, Z))
    return jax.shard_map(
        functools.partial(per_device, mesh.shape["model"]),
        mesh=split,
        in_specs=(P(FSDP, Z),) * 9 + (P((*FSDP, Z)),) * 2,
        out_specs=(P(None, Z),) * 3 + (P(Z),) * 3 + (P(),) + (P(FSDP, Z),) * 3,
        check_vma=False,
    )
```

profile of v0, /device:TPU:1, one launch (start us, length us, event | category | flops | bytes accessed | tf_op | source)
XLA Modules:
  0.0 78.4 jit_solution(10607899681610158184)
XLA Ops:
  0.6 2.0 %encode.1 = (f32[40,512]{1,0:T(8,128)S(1)}, f32[40,128]{1,0:T(8,128)S(1)}, f32[40,128]{1,0:T(8,128)S(1)}, bf16[8,256,128]{2,1,0:T(8,128)(2,1)S(1)}) custom-call(f32[5]{0:T(128)} %norm_train.1, f32[5]{0:T(128)} %norm_step.1, f32[40,512]{1,0:T(8,128)} %refs_0_.1, f32[40,512]{1,0:T(8,128)} %refs_1_.1, f32[40,512]{1,0:T(8,128)} %refs_2_.1, f32[40,128]{1,0:T(8,128)} %refs_3_.1, ...), custom_call_target="tpu_custom_call" | custom-call | tf_op jit(solution)/shard_map/encode/pallas_call | solution.py:91
  2.6 25.0 %all_to_all.10.refs_0_.own = bf16[8,256,128]{2,1,0:T(8,128)(2,1)S(1)} all-to-all(bf16[8,256,128]{2,1,0:T(8,128)(2,1)S(1)} %get-tuple-element.20), channel_id=1, replica_groups={{0,96,128,224,256,352,384,480},{16,112,144,240,272,368,400,496},{32,64,..., dimensions={0} | all-to-all | bytes 1048576 | tf_op jit(solution)/shard_map/all_to_all | solution.py:271
  27.6 2.2 %collective-permute-start.2 = (bf16[8,256,128]{2,1,0:T(8,128)(2,1)S(1)}, bf16[8,256,128]{2,1,0:T(8,128)(2,1)S(1)}, u32[]{:S(2)}, u32[]{:S(2)}) collective-permute-start(bf16[8,256,128]{2,1,0:T(8,128)(2,1)S(1)} %all_to_all.10.refs_0_.own), channel_id=1, source_target_pairs={{48,0},{56,8},{0,16},{8,24},{16,32},{24,40},{32,48},{40,56},{112,6... | collective-permute-start | bytes 1572872 | tf_op jit(solution)/shard_map/ppermute | solution.py:262
  29.8 3.9 %collective-permute-start.1 = (bf16[8,256,128]{2,1,0:T(8,128)(2,1)S(1)}, bf16[8,256,128]{2,1,0:T(8,128)(2,1)S(1)}, u32[]{:S(2)}, u32[]{:S(2)}) collective-permute-start(bf16[8,256,128]{2,1,0:T(8,128)(2,1)S(1)} %all_to_all.10.refs_0_.own), channel_id=1, source_target_pairs={{64,0},{456,8},{80,16},{472,24},{96,32},{488,40},{112,48},{504,56}... | collective-permute-start | bytes 1572872 | tf_op jit(solution)/shard_map/ppermute | solution.py:262
  33.7 4.3 %collective-permute-start = (bf16[8,256,128]{2,1,0:T(8,128)(2,1)S(1)}, bf16[8,256,128]{2,1,0:T(8,128)(2,1)S(1)}, u32[]{:S(2)}, u32[]{:S(2)}) collective-permute-start(bf16[8,256,128]{2,1,0:T(8,128)(2,1)S(1)} %all_to_all.10.refs_0_.own), channel_id=1, source_target_pairs={{16,0},{24,8},{32,16},{40,24},{48,32},{56,40},{0,48},{8,56},{80,64... | collective-permute-start | bytes 1572872 | tf_op jit(solution)/shard_map/ppermute | solution.py:262
  38.0 3.6 %collective-permute-done.2.refs_3_ = bf16[8,256,128]{2,1,0:T(8,128)(2,1)S(1)} collective-permute-done((bf16[8,256,128]{2,1,0:T(8,128)(2,1)S(1)}, bf16[8,256,128]{2,1,0:T(8,128)(2,1)S(1)}, u32[]{:S(2)}, u32[]{:S(2)}) %collective-permute-start.2) | collective-permute-done | bytes 524320 | tf_op jit(solution)/shard_map/ppermute | solution.py:262
  41.6 0.0 collective-permute-done.1.refs_2_
  41.6 6.8 %collective-permute-done.refs_1_ = bf16[8,256,128]{2,1,0:T(8,128)(2,1)S(1)} collective-permute-done((bf16[8,256,128]{2,1,0:T(8,128)(2,1)S(1)}, bf16[8,256,128]{2,1,0:T(8,128)(2,1)S(1)}, u32[]{:S(2)}, u32[]{:S(2)}) %collective-permute-start) | collective-permute-done | bytes 524320 | tf_op jit(solution)/shard_map/ppermute | solution.py:262
  48.4 0.1 pack.1.refs_0_
  48.5 3.6 %collective-permute-start.3 = (bf16[4,8,256,128]{3,2,1,0:T(8,128)(2,1)S(1)}, bf16[4,8,256,128]{3,2,1,0:T(8,128)(2,1)}, u32[]{:S(2)}, u32[]{:S(2)}) collective-permute-start(bf16[4,8,256,128]{3,2,1,0:T(8,128)(2,1)S(1)} %pack.1.refs_0_), channel_id=1, source_target_pairs={{8,0},{0,8},{24,16},{16,24},{40,32},{32,40},{56,48},{48,56},{72,64... | collective-permute-start | bytes 6291464 | tf_op jit(solution)/shard_map/ppermute | solution.py:262
  52.2 0.7 prepare.1
  52.9 14.1 %all-to-all-start.1 = ((bf16[64,8,128]{2,1,0:T(8,128)(2,1)}), bf16[64,8,128]{2,1,0:T(8,128)(2,1)S(1)}, u32[]{:S(2)}, u32[]{:S(2)}) async-start(bf16[64,8,128]{2,1,0:T(8,128)(2,1)} %prepare.1), calls=%async_computation.1 | async-start | bytes 262144 | tf_op jit(solution)/shard_map/all_to_all | solution.py:286
  67.0 0.6 copy.22
  67.6 0.6 copy.23
  68.2 0.6 copy.21
  68.8 0.0 collective-permute-done.3.refs_1_
  68.8 4.5 %decode.1 = (bf16[8,4,2,40,512]{4,3,2,1,0:T(8,128)(2,1)}, bf16[8,4,2,40,128]{4,3,2,1,0:T(8,128)(2,1)}, bf16[8,4,2,40,128]{4,3,2,1,0:T(8,128)(2,1)}, f32[1,512]{1...) custom-call(bf16[4,8,256,128]{3,2,1,0:T(8,128)(2,1)S(1)} %pack.1.refs_0_, ...), custom_call_target="tpu_custom_call" | custom-call | tf_op jit(solution)/shard_map/decode/pallas_call | solution.py:207
  73.4 3.6 %all-to-all-done.1 = bf16[64,8,128]{2,1,0:T(8,128)(2,1)S(1)} async-done(((bf16[64,8,128]{2,1,0:T(8,128)(2,1)}), bf16[64,8,128]{2,1,0:T(8,128)(2,1)S(1)}, u32[]{:S(2)}, u32[]{:S(2)}) %all-to-all-start.1) | async-done | bytes 131104 | tf_op jit(solution)/shard_map/all_to_all | solution.py:286
  76.9 0.0 copy-start
  76.9 0.7 copy-done
  77.6 0.8 %gather_norm.1 = bf16[20,128]{1,0:T(8,128)(2,1)} custom-call(bf16[4,2,8,8,128]{4,3,2,1,0:T(8,128)(2,1)S(1)} %bitcast.8, f32[1,512]{1,0:T(1,128)S(1)} %copy-done), custom_call_target="tpu_custom_call" | custom-call | tf_op jit(solution)/shard_map/gather_norm/pallas_call | solution.py:244
Async XLA Ops:
  27.6 14.0 %collective-permute-start.2 = (bf16[8,256,128]{2,1,0:T(8,128)(2,1)S(1)}, bf16[8,256,128]{2,1,0:T(8,128)(2,1)S(1)}, u32[]{:S(2)}, u32[]{:S(2)}) collective-permute-start(bf16[8,256,128]{2,1,0:T(8,128)(2,1)S(1)} %all_to_all.10.refs_0_.own), channel_id=1, source_target_pairs={{48,0},{56,8},{0,16},{8,24},{16,32},{24,40},{32,48},{40,56},{112,6... | collective-permute-start | bytes 1572872 | tf_op jit(solution)/shard_map/ppermute | solution.py:262
  29.8 11.7 %collective-permute-start.1 = (bf16[8,256,128]{2,1,0:T(8,128)(2,1)S(1)}, bf16[8,256,128]{2,1,0:T(8,128)(2,1)S(1)}, u32[]{:S(2)}, u32[]{:S(2)}) collective-permute-start(bf16[8,256,128]{2,1,0:T(8,128)(2,1)S(1)} %all_to_all.10.refs_0_.own), channel_id=1, source_target_pairs={{64,0},{456,8},{80,16},{472,24},{96,32},{488,40},{112,48},{504,56}... | collective-permute-start | bytes 1572872 | tf_op jit(solution)/shard_map/ppermute | solution.py:262
  33.7 14.7 %collective-permute-start = (bf16[8,256,128]{2,1,0:T(8,128)(2,1)S(1)}, bf16[8,256,128]{2,1,0:T(8,128)(2,1)S(1)}, u32[]{:S(2)}, u32[]{:S(2)}) collective-permute-start(bf16[8,256,128]{2,1,0:T(8,128)(2,1)S(1)} %all_to_all.10.refs_0_.own), channel_id=1, source_target_pairs={{16,0},{24,8},{32,16},{40,24},{48,32},{56,40},{0,48},{8,56},{80,64... | collective-permute-start | bytes 1572872 | tf_op jit(solution)/shard_map/ppermute | solution.py:262
  48.5 20.3 %collective-permute-start.3 = (bf16[4,8,256,128]{3,2,1,0:T(8,128)(2,1)S(1)}, bf16[4,8,256,128]{3,2,1,0:T(8,128)(2,1)}, u32[]{:S(2)}, u32[]{:S(2)}) collective-permute-start(bf16[4,8,256,128]{3,2,1,0:T(8,128)(2,1)S(1)} %pack.1.refs_0_), channel_id=1, source_target_pairs={{8,0},{0,8},{24,16},{16,24},{40,32},{32,40},{56,48},{48,56},{72,64... | collective-permute-start | bytes 6291464 | tf_op jit(solution)/shard_map/ppermute | solution.py:262
  52.9 24.1 %all-to-all-start.1 = ((bf16[64,8,128]{2,1,0:T(8,128)(2,1)}), bf16[64,8,128]{2,1,0:T(8,128)(2,1)S(1)}, u32[]{:S(2)}, u32[]{:S(2)}) async-start(bf16[64,8,128]{2,1,0:T(8,128)(2,1)} %prepare.1), calls=%async_computation.1 | async-start | bytes 262144 | tf_op jit(solution)/shard_map/all_to_all | solution.py:286
  76.9 0.7 copy-start
where the time goes:
time: 78.8 us; the launch traced here: 78.4 us
  starting transfers between devices  28.1 us (36%)
  blocking collectives  25 us (32%)
  waiting for transfers between devices  14 us (18%)
  Pallas kernels  8.08 us (10%)
  local copies, waits for them, and re-layouts  2.53 us (3%)
    all_to_all x1, blocking collectives, per_device(): lax.all_to_all(wire, FSDP, 0, 0, axis_index_groups=same_kind, tiled=True)  25 us
    all_to_all x1, starting transfers between devices, per_device(): lax.all_to_all(gain, FSDP + (Z,), 0, 0, axis_index_groups=rest, tiled=True)  14.1 us
    ppermute x4, starting transfers between devices, come_from(): lax.ppermute(value, FSDP, [(place(*source(*s)), place(*s)) for s in SPOTS])  14 us
    ppermute x4, waiting for transfers between devices, come_from(): lax.ppermute(value, FSDP, [(place(*source(*s)), place(*s)) for s in SPOTS])  10.4 us
    pallas_call x1, Pallas kernels, decode(): pl.pallas_call(functools.partial(decode_kernel, widths, rows), out_shape=...  4.51 us
    all_to_all x1, waiting for transfers between devices, per_device(): lax.all_to_all(gain, FSDP + (Z,), 0, 0, axis_index_groups=rest, tiled=True)  3.58 us
    unnamed x5, local copies, waits for them, and re-layouts  2.53 us
    pallas_call x1, Pallas kernels, encode(): pl.pallas_call(functools.partial(encode_kernel, widths), out_shape=out, i...  1.96 us
  transfers between devices with their start and end apart: 5, of which 3 were waited for; matrix products, arithmetic and copies ran while one was open for 2% of the time, Pallas kernels for 7%

commit v1 on v0

--- a/solution.py
+++ b/solution.py
@@ -31,12 +31,17 @@
     return tuple(lax.axis_index(a) for a in (Y, X, C))
 
 
-def encode_kernel(widths, norm_train, norm_step, *refs):
+def encode_kernel(widths, *refs):
     n = len(widths)
+    norms, refs = refs[:2], refs[2:]
     sources, fresh_refs, wire = refs[: 3 * n], refs[3 * n : 4 * n], refs[4 * n]
-    ins, sems = refs[4 * n + 1 : -1], refs[-1]
+    ins, (norm_train, norm_step, sems) = refs[4 * n + 1 : -3], refs[-3:]
     loads = [pltpu.make_async_copy(s, d, sems.at[i]) for i, (s, d) in enumerate(zip(sources, ins))]
-    for load in loads:
+    few_loads = [
+        pltpu.make_async_copy(s, d, sems.at[3 * n + i])
+        for i, (s, d) in enumerate(zip(norms, (norm_train, norm_step)))
+    ]
+    for load in loads + few_loads:
         load.start()
     copies = wire.shape[0]
     rows = ins[0].shape[0]
@@ -74,6 +79,8 @@
     lane = lax.broadcasted_iota(jnp.int32, (1, LANES), 1) - lax.rem(start, LANES)
     lane = jnp.where(lane < 0, lane + LANES, lane)
     gain = jnp.zeros((1, LANES), jnp.float32)
+    for load in few_loads:
+        load.wait()
     for i in range(few):
         gain = jnp.where(lane == i, norm_train[i] + norm_step[i], gain)
     gain = gain.astype(jnp.bfloat16)
@@ -91,11 +98,11 @@
     return pl.pallas_call(
         functools.partial(encode_kernel, widths),
         out_shape=out,
-        in_specs=[pl.BlockSpec(memory_space=pltpu.SMEM)] * 2
-        + [pl.BlockSpec(memory_space=pltpu.HBM)] * len(arrays),
+        in_specs=[pl.BlockSpec(memory_space=pltpu.HBM)] * (2 + len(arrays)),
         out_specs=[vmem] * len(out),
         scratch_shapes=[pltpu.VMEM(a.shape, a.dtype) for a in arrays]
-        + [pltpu.SemaphoreType.DMA((len(arrays),))],
+        + [pltpu.SMEM(a.shape, a.dtype) for a in norms]
+        + [pltpu.SemaphoreType.DMA((len(arrays) + 2,))],
         compiler_params=pltpu.CompilerParams(vmem_limit_bytes=16 * 2**20),
         name="encode",
     )(*(in_hbm(a) for a in norms), *(in_hbm(a) for a in arrays))
@@ -178,8 +185,8 @@
 
     def body(y, _):
         for i, wire in enumerate(wires):
-            x = lax.rem(kind + i % 4 + 2 * y, NX)
             c = mine if i < 4 else 1 - mine
+            x = lax.rem(kind + (0, 1 + 2 * c, 2, 3 - 2 * c)[i % 4] + 2 * y, NX)
             slab = 0
             for at, width in enumerate(widths):
                 for k in range(width // LANES):
@@ -244,11 +251,11 @@
     return pl.pallas_call(
         norm_kernel,
         out_shape=jax.ShapeDtypeStruct((NY * NX * 2 * few // LANES, LANES), jnp.bfloat16),
-        in_specs=[pl.BlockSpec(memory_space=pltpu.VMEM)] * 2,
+        in_specs=[pl.BlockSpec(memory_space=pltpu.VMEM), pl.BlockSpec(memory_space=pltpu.HBM)],
         out_specs=pl.BlockSpec(memory_space=pltpu.VMEM),
         compiler_params=pltpu.CompilerParams(vmem_limit_bytes=4 * 2**20),
         name="gather_norm",
-    )(gains, after)
+    )(gains, in_hbm(after))
 
 
 def place(y, x, c):
@@ -269,8 +276,8 @@
     *fresh, wire = encode(NY, norms, arrays)
     same_kind = [[place(y, k - 2 * y, c) for y in range(NY)] for c in range(2) for k in range(NX)]
     own = lax.all_to_all(wire, FSDP, 0, 0, axis_index_groups=same_kind, tiled=True)
-    up = come_from(own, lambda y, x, c: (y, x + 1, c))
-    down = come_from(own, lambda y, x, c: (y, x - 1, c))
+    up = come_from(own, lambda y, x, c: (y, x + 1 - 2 * c, c))
+    down = come_from(own, lambda y, x, c: (y, x - 1 + 2 * c, c))
     side = come_from(own, lambda y, x, c: (y + 1 - 2 * c, x, c))
     used = sum(w // LANES for w in widths) * (rows + PARTS)
     gain = prepare(used, NX * 2 * n_z, own)

time: 78.8 us -> 73.3 us (0.930)
  starting transfers between devices: 28.1 us -> 23.7 us
    ppermute x4, starting transfers between devices: 14 us -> 11.1 us  [come_from(): lax.ppermute(value, FSDP, [(place(*source(*s)), place(*s)) for s in SPOTS])]
    all_to_all x1, starting transfers between devices: 14.1 us -> 12.6 us  [per_device(): lax.all_to_all(gain, FSDP + (Z,), 0, 0, axis_index_groups=rest, tiled=True)]
    unnamed x5 -> x3, local copies, waits for them, and re-layouts: 2.53 us -> 1.85 us
  transfers between devices with their start and end apart: 5 -> 5, of which waited for: 3 -> 4; matrix products, arithmetic and copies ran while one was open for 2% -> 3% of each run, Pallas kernels for 7% -> 7%
where the time goes in v1:
time: 73.3 us; the launch traced here: 72.8 us
  blocking collectives  25 us (34%)
  starting transfers between devices  23.7 us (32%)
  waiting for transfers between devices  14.2 us (19%)
  Pallas kernels  7.45 us (10%)
  local copies, waits for them, and re-layouts  1.85 us (3%)
    all_to_all x1, blocking collectives, per_device(): lax.all_to_all(wire, FSDP, 0, 0, axis_index_groups=same_kind, tiled=True)  25 us
    all_to_all x1, starting transfers between devices, per_device(): lax.all_to_all(gain, FSDP + (Z,), 0, 0, axis_index_groups=rest, tiled=True)  12.6 us
    ppermute x4, starting transfers between devices, come_from(): lax.ppermute(value, FSDP, [(place(*source(*s)), place(*s)) for s in SPOTS])  11.1 us
    ppermute x4, waiting for transfers between devices, come_from(): lax.ppermute(value, FSDP, [(place(*source(*s)), place(*s)) for s in SPOTS])  10.6 us
    pallas_call x1, Pallas kernels, decode(): pl.pallas_call(functools.partial(decode_kernel, widths, rows), out_shape=...  4.51 us
    all_to_all x1, waiting for transfers between devices, per_device(): lax.all_to_all(gain, FSDP + (Z,), 0, 0, axis_index_groups=rest, tiled=True)  3.58 us
    unnamed x3, local copies, waits for them, and re-layouts  1.85 us
  transfers between devices with their start and end apart: 5, of which 4 were waited for; matrix products, arithmetic and copies ran while one was open for 3% of the time, Pallas kernels for 7%

profile of v1, /device:TPU:1, one launch (start us, length us, event | category | flops | bytes accessed | tf_op | source)
XLA Modules:
  0.0 72.8 jit_solution(16040304539018246724)
XLA Ops:
  0.6 1.3 %encode.1 = (f32[40,512]{1,0:T(8,128)S(1)}, f32[40,128]{1,0:T(8,128)S(1)}, f32[40,128]{1,0:T(8,128)S(1)}, bf16[8,256,128]{2,1,0:T(8,128)(2,1)S(1)}) custom-call(f32[5]{0:T(128)} %refs_0_.1, f32[5]{0:T(128)} %refs_1_.1, f32[40,512]{1,0:T(8,128)} %refs_2_.1, f32[40,512]{1,0:T(8,128)} %refs_3_.1, f32[40,512]{1,0:T(8,128)} %refs_4_.1, f32[40,128]{1,0:T(8,128)} %refs_5_.1, ...), custom_call_target="tpu_custom_call" | custom-call | tf_op jit(solution)/shard_map/encode/pallas_call | solution.py:98
  2.0 25.0 %all_to_all.10.refs_0_.own = bf16[8,256,128]{2,1,0:T(8,128)(2,1)S(1)} all-to-all(bf16[8,256,128]{2,1,0:T(8,128)(2,1)S(1)} %get-tuple-element.20), channel_id=1, replica_groups={{0,96,128,224,256,352,384,480},{16,112,144,240,272,368,400,496},{32,64,..., dimensions={0} | all-to-all | bytes 1048576 | tf_op jit(solution)/shard_map/all_to_all | solution.py:278
  27.0 3.1 %collective-permute-start.2 = (bf16[8,256,128]{2,1,0:T(8,128)(2,1)S(1)}, bf16[8,256,128]{2,1,0:T(8,128)(2,1)S(1)}, u32[]{:S(2)}, u32[]{:S(2)}) collective-permute-start(bf16[8,256,128]{2,1,0:T(8,128)(2,1)S(1)} %all_to_all.10.refs_0_.own), channel_id=1, source_target_pairs={{48,0},{24,8},{0,16},{40,24},{16,32},{56,40},{32,48},{8,56},{112,6... | collective-permute-start | bytes 1572872 | tf_op jit(solution)/shard_map/ppermute | solution.py:269
  30.1 3.6 %collective-permute-start.1 = (bf16[8,256,128]{2,1,0:T(8,128)(2,1)S(1)}, bf16[8,256,128]{2,1,0:T(8,128)(2,1)S(1)}, u32[]{:S(2)}, u32[]{:S(2)}) collective-permute-start(bf16[8,256,128]{2,1,0:T(8,128)(2,1)S(1)} %all_to_all.10.refs_0_.own), channel_id=1, source_target_pairs={{64,0},{456,8},{80,16},{472,24},{96,32},{488,40},{112,48},{504,56}... | collective-permute-start | bytes 1572872 | tf_op jit(solution)/shard_map/ppermute | solution.py:269
  33.7 2.5 %collective-permute-start = (bf16[8,256,128]{2,1,0:T(8,128)(2,1)S(1)}, bf16[8,256,128]{2,1,0:T(8,128)(2,1)S(1)}, u32[]{:S(2)}, u32[]{:S(2)}) collective-permute-start(bf16[8,256,128]{2,1,0:T(8,128)(2,1)S(1)} %all_to_all.10.refs_0_.own), channel_id=1, source_target_pairs={{16,0},{56,8},{32,16},{8,24},{48,32},{24,40},{0,48},{40,56},{80,64... | collective-permute-start | bytes 1572872 | tf_op jit(solution)/shard_map/ppermute | solution.py:269
  36.2 1.0 %collective-permute-done.2.refs_3_ = bf16[8,256,128]{2,1,0:T(8,128)(2,1)S(1)} collective-permute-done((bf16[8,256,128]{2,1,0:T(8,128)(2,1)S(1)}, bf16[8,256,128]{2,1,0:T(8,128)(2,1)S(1)}, u32[]{:S(2)}, u32[]{:S(2)}) %collective-permute-start.2) | collective-permute-done | bytes 524320 | tf_op jit(solution)/shard_map/ppermute | solution.py:269
  37.2 4.3 %collective-permute-done.1.refs_2_ = bf16[8,256,128]{2,1,0:T(8,128)(2,1)S(1)} collective-permute-done((bf16[8,256,128]{2,1,0:T(8,128)(2,1)S(1)}, bf16[8,256,128]{2,1,0:T(8,128)(2,1)S(1)}, u32[]{:S(2)}, u32[]{:S(2)}) %collective-permute-start.1) | collective-permute-done | bytes 524320 | tf_op jit(solution)/shard_map/ppermute | solution.py:269
  41.5 5.2 %collective-permute-done.refs_1_ = bf16[8,256,128]{2,1,0:T(8,128)(2,1)S(1)} collective-permute-done((bf16[8,256,128]{2,1,0:T(8,128)(2,1)S(1)}, bf16[8,256,128]{2,1,0:T(8,128)(2,1)S(1)}, u32[]{:S(2)}, u32[]{:S(2)}) %collective-permute-start) | collective-permute-done | bytes 524320 | tf_op jit(solution)/shard_map/ppermute | solution.py:269
  46.8 0.1 pack.1.refs_0_
  46.9 1.9 %collective-permute-start.3 = (bf16[4,8,256,128]{3,2,1,0:T(8,128)(2,1)S(1)}, bf16[4,8,256,128]{3,2,1,0:T(8,128)(2,1)}, u32[]{:S(2)}, u32[]{:S(2)}) collective-permute-start(bf16[4,8,256,128]{3,2,1,0:T(8,128)(2,1)S(1)} %pack.1.refs_0_), channel_id=1, source_target_pairs={{8,0},{0,8},{24,16},{16,24},{40,32},{32,40},{56,48},{48,56},{72,64... | collective-permute-start | bytes 6291464 | tf_op jit(solution)/shard_map/ppermute | solution.py:269
  48.8 0.7 prepare.1
  49.5 12.6 %all-to-all-start.1 = ((bf16[64,8,128]{2,1,0:T(8,128)(2,1)}), bf16[64,8,128]{2,1,0:T(8,128)(2,1)S(1)}, u32[]{:S(2)}, u32[]{:S(2)}) async-start(bf16[64,8,128]{2,1,0:T(8,128)(2,1)} %prepare.1), calls=%async_computation.1 | async-start | bytes 262144 | tf_op jit(solution)/shard_map/all_to_all | solution.py:293
  62.1 0.6 copy.22
  62.7 0.6 copy.23
  63.3 0.6 copy.21
  63.9 0.0 collective-permute-done.3.refs_1_
  63.9 4.5 %decode.1 = (bf16[8,4,2,40,512]{4,3,2,1,0:T(8,128)(2,1)}, bf16[8,4,2,40,128]{4,3,2,1,0:T(8,128)(2,1)}, bf16[8,4,2,40,128]{4,3,2,1,0:T(8,128)(2,1)}, f32[1,512]{1...) custom-call(bf16[4,8,256,128]{3,2,1,0:T(8,128)(2,1)S(1)} %pack.1.refs_0_, ...), custom_call_target="tpu_custom_call" | custom-call | tf_op jit(solution)/shard_map/decode/pallas_call | solution.py:214
  68.4 3.6 %all-to-all-done.1 = bf16[64,8,128]{2,1,0:T(8,128)(2,1)S(1)} async-done(((bf16[64,8,128]{2,1,0:T(8,128)(2,1)}), bf16[64,8,128]{2,1,0:T(8,128)(2,1)S(1)}, u32[]{:S(2)}, u32[]{:S(2)}) %all-to-all-start.1) | async-done | bytes 131104 | tf_op jit(solution)/shard_map/all_to_all | solution.py:293
  72.0 0.8 %gather_norm.1 = bf16[20,128]{1,0:T(8,128)(2,1)} custom-call(bf16[4,2,8,8,128]{4,3,2,1,0:T(8,128)(2,1)S(1)} %bitcast.8, f32[1,512]{1,0:T(1,128)} %get-tuple-element.24._), custom_call_target="tpu_custom_call" | custom-call | tf_op jit(solution)/shard_map/gather_norm/pallas_call | solution.py:251
Async XLA Ops:
  27.0 10.2 %collective-permute-start.2 = (bf16[8,256,128]{2,1,0:T(8,128)(2,1)S(1)}, bf16[8,256,128]{2,1,0:T(8,128)(2,1)S(1)}, u32[]{:S(2)}, u32[]{:S(2)}) collective-permute-start(bf16[8,256,128]{2,1,0:T(8,128)(2,1)S(1)} %all_to_all.10.refs_0_.own), channel_id=1, source_target_pairs={{48,0},{24,8},{0,16},{40,24},{16,32},{56,40},{32,48},{8,56},{112,6... | collective-permute-start | bytes 1572872 | tf_op jit(solution)/shard_map/ppermute | solution.py:269
  30.1 11.4 %collective-permute-start.1 = (bf16[8,256,128]{2,1,0:T(8,128)(2,1)S(1)}, bf16[8,256,128]{2,1,0:T(8,128)(2,1)S(1)}, u32[]{:S(2)}, u32[]{:S(2)}) collective-permute-start(bf16[8,256,128]{2,1,0:T(8,128)(2,1)S(1)} %all_to_all.10.refs_0_.own), channel_id=1, source_target_pairs={{64,0},{456,8},{80,16},{472,24},{96,32},{488,40},{112,48},{504,56}... | collective-permute-start | bytes 1572872 | tf_op jit(solution)/shard_map/ppermute | solution.py:269
  33.7 13.1 %collective-permute-start = (bf16[8,256,128]{2,1,0:T(8,128)(2,1)S(1)}, bf16[8,256,128]{2,1,0:T(8,128)(2,1)S(1)}, u32[]{:S(2)}, u32[]{:S(2)}) collective-permute-start(bf16[8,256,128]{2,1,0:T(8,128)(2,1)S(1)} %all_to_all.10.refs_0_.own), channel_id=1, source_target_pairs={{16,0},{56,8},{32,16},{8,24},{48,32},{24,40},{0,48},{40,56},{80,64... | collective-permute-start | bytes 1572872 | tf_op jit(solution)/shard_map/ppermute | solution.py:269
  46.9 17.0 %collective-permute-start.3 = (bf16[4,8,256,128]{3,2,1,0:T(8,128)(2,1)S(1)}, bf16[4,8,256,128]{3,2,1,0:T(8,128)(2,1)}, u32[]{:S(2)}, u32[]{:S(2)}) collective-permute-start(bf16[4,8,256,128]{3,2,1,0:T(8,128)(2,1)S(1)} %pack.1.refs_0_), channel_id=1, source_target_pairs={{8,0},{0,8},{24,16},{16,24},{40,32},{32,40},{56,48},{48,56},{72,64... | collective-permute-start | bytes 6291464 | tf_op jit(solution)/shard_map/ppermute | solution.py:269
  49.5 22.5 %all-to-all-start.1 = ((bf16[64,8,128]{2,1,0:T(8,128)(2,1)}), bf16[64,8,128]{2,1,0:T(8,128)(2,1)S(1)}, u32[]{:S(2)}, u32[]{:S(2)}) async-start(bf16[64,8,128]{2,1,0:T(8,128)(2,1)} %prepare.1), calls=%async_computation.1 | async-start | bytes 262144 | tf_op jit(solution)/shard_map/all_to_all | solution.py:293

commit v2 on v1

--- a/solution.py
+++ b/solution.py
@@ -69,10 +69,10 @@
             for c in range(copies):
                 wire[c, slab * rows : (slab + 1) * rows, :] = code
                 for p, part in enumerate(parts):
-                    row = slabs * rows + p * slabs + slab
+                    row = slabs * rows + p * 8 + slab
                     wire[c, row : row + 1, :] = part
             slab += 1
-    used = slabs * (rows + PARTS)
+    used = slabs * rows + 7
     few = norm_train.shape[0]
     y, x, c = spot()
     start = (place(y, x, c) * lax.axis_size(Z) + lax.axis_index(Z)) * few
@@ -93,7 +93,7 @@
     widths = tuple(a.shape[1] for a in arrays[::3])
     slabs = sum(w // LANES for w in widths)
     out = [pltpu.VMEM(a.shape, a.dtype) for a in arrays[::3]]
-    out.append(pltpu.VMEM((copies, padded(slabs * (rows + PARTS) + 1), LANES), jnp.bfloat16))
+    out.append(pltpu.VMEM((copies, slabs * rows + PARTS * 8, LANES), jnp.bfloat16))
     vmem = pl.BlockSpec(memory_space=pltpu.VMEM)
     return pl.pallas_call(
         functools.partial(encode_kernel, widths),
@@ -164,10 +164,9 @@
     kind = lax.rem(x + 2 * y, NX)
     best = None
     for i, wire in enumerate(wires):
-        tail = wire[:, low:, :].astype(jnp.float32)
-        scale = tail[:, :slabs]
+        scale = wire[:, low : low + 8, :].astype(jnp.float32)
         for p in range(1, PARTS):
-            scale = scale + tail[:, p * slabs : (p + 1) * slabs]
+            scale = scale + wire[:, low + 8 * p : low + 8 * (p + 1), :].astype(jnp.float32)
         ratios[i] = scale
         top = jnp.max(scale, axis=0)
         best = top if best is None else jnp.maximum(best, top)
@@ -180,8 +179,8 @@
     for i in range(8):
         ratios[i] = ratios[i] * share
 
-    def copy(at, y):
-        return pltpu.make_async_copy(stage[at].at[y], serve[at].at[y], sems.at[at, y])
+    def copy(at, part):
+        return pltpu.make_async_copy(stage[at].at[part], serve[at].at[part], sems.at[at])
 
     def body(y, _):
         for i, wire in enumerate(wires):
@@ -201,14 +200,12 @@
 
     lax.fori_loop(0, NY, body, 0)
     for at in range(n):
-        for y in range(NY):
-            copy(at, y).wait()
+        copy(at, slice(None)).wait()
 
 
 def decode(widths, rows, own, other):
     stage = [(NY, NX, 2, rows, w) for w in widths]
     vmem = pl.BlockSpec(memory_space=pltpu.VMEM)
-    slabs = sum(w // LANES for w in widths)
     out = [jax.ShapeDtypeStruct(s, jnp.bfloat16) for s in stage]
     out += [jax.ShapeDtypeStruct((1, w), jnp.float32) for w in widths]
     return pl.pallas_call(
@@ -218,8 +215,8 @@
         out_specs=[pl.BlockSpec(memory_space=pl.ANY)] * len(widths) + [vmem] * len(widths),
         scratch_shapes=[pltpu.VMEM(s, jnp.bfloat16) for s in stage]
         + [
-            pltpu.VMEM((8, NY, slabs, LANES), jnp.float32),
-            pltpu.SemaphoreType.DMA((len(widths), NY)),
+            pltpu.VMEM((8, NY, 8, LANES), jnp.float32),
+            pltpu.SemaphoreType.DMA((len(widths),)),
         ],
         compiler_params=pltpu.CompilerParams(vmem_limit_bytes=16 * 2**20),
         name="decode",
@@ -279,17 +276,22 @@
     up = come_from(own, lambda y, x, c: (y, x + 1 - 2 * c, c))
     down = come_from(own, lambda y, x, c: (y, x - 1 + 2 * c, c))
     side = come_from(own, lambda y, x, c: (y + 1 - 2 * c, x, c))
-    used = sum(w // LANES for w in widths) * (rows + PARTS)
+    used = sum(w // LANES for w in widths) * rows + 7
     gain = prepare(used, NX * 2 * n_z, own)
-    rest = [
-        [
-            (place(y, k - 2 * y, c) * n_z) + z
-            for k in range(NX)
-            for c in range(2)
-            for z in range(n_z)
-        ]
-        for y in range(NY)
-    ]
+    rest = []
+    for y in range(0, NY, 2):
+        for x in range(0, NX, 2):
+            square = sorted(
+                ((x + j + 2 * (y + i)) % NX, y + i, x + j) for i in range(2) for j in range(2)
+            )
+            rest.append(
+                [
+                    place(at_y, at_x, c) * n_z + z
+                    for _, at_y, at_x in square
+                    for c in range(2)
+                    for z in range(n_z)
+                ]
+            )
     gains = lax.all_to_all(gain, FSDP + (Z,), 0, 0, axis_index_groups=rest, tiled=True)
     gains = gains.reshape(NX, 2, n_z, NY, LANES)
     own = pack((own, up, side, down))

time: 73.3 us -> 72.1 us (0.984)
  no operation moved by 1% of the time
where the time goes in v2:
time: 72.1 us; the launch traced here: 71.3 us
  blocking collectives  25 us (35%)
  starting transfers between devices  23.1 us (32%)
  waiting for transfers between devices  13.5 us (19%)
  Pallas kernels  7.23 us (10%)
  local copies, waits for them, and re-layouts  1.85 us (3%)
    all_to_all x1, blocking collectives, per_device(): lax.all_to_all(wire, FSDP, 0, 0, axis_index_groups=same_kind, tiled=True)  25 us
    all_to_all x1, starting transfers between devices, per_device(): lax.all_to_all(gain, FSDP + (Z,), 0, 0, axis_index_groups=rest, tiled=True)  12 us
    ppermute x4, starting transfers between devices, come_from(): lax.ppermute(value, FSDP, [(place(*source(*s)), place(*s)) for s in SPOTS])  11.1 us
    ppermute x4, waiting for transfers between devices, come_from(): lax.ppermute(value, FSDP, [(place(*source(*s)), place(*s)) for s in SPOTS])  10.6 us
    pallas_call x1, Pallas kernels, decode(): pl.pallas_call(functools.partial(decode_kernel, widths, rows), out_shape=...  4.29 us
    all_to_all x1, waiting for transfers between devices, per_device(): lax.all_to_all(gain, FSDP + (Z,), 0, 0, axis_index_groups=rest, tiled=True)  2.88 us
    unnamed x3, local copies, waits for them, and re-layouts  1.85 us
  transfers between devices with their start and end apart: 5, of which 4 were waited for; matrix products, arithmetic and copies ran while one was open for 3% of the time, Pallas kernels for 7%

profile of v2, /device:TPU:1, one launch (start us, length us, event | category | flops | bytes accessed | tf_op | source)
XLA Modules:
  0.0 71.3 jit_solution(10007706519902013944)
XLA Ops:
  0.6 1.3 %encode.1 = (f32[40,512]{1,0:T(8,128)S(1)}, f32[40,128]{1,0:T(8,128)S(1)}, f32[40,128]{1,0:T(8,128)S(1)}, bf16[8,256,128]{2,1,0:T(8,128)(2,1)S(1)}) custom-call(f32[5]{0:T(128)} %refs_0_.1, f32[5]{0:T(128)} %refs_1_.1, f32[40,512]{1,0:T(8,128)} %refs_2_.1, f32[40,512]{1,0:T(8,128)} %refs_3_.1, f32[40,512]{1,0:T(8,128)} %refs_4_.1, f32[40,128]{1,0:T(8,128)} %refs_5_.1, ...), custom_call_target="tpu_custom_call" | custom-call | tf_op jit(solution)/shard_map/encode/pallas_call | solution.py:98
  2.0 25.0 %all_to_all.10.refs_0_.own = bf16[8,256,128]{2,1,0:T(8,128)(2,1)S(1)} all-to-all(bf16[8,256,128]{2,1,0:T(8,128)(2,1)S(1)} %get-tuple-element.20), channel_id=1, replica_groups={{0,96,128,224,256,352,384,480},{16,112,144,240,272,368,400,496},{32,64,..., dimensions={0} | all-to-all | bytes 1048576 | tf_op jit(solution)/shard_map/all_to_all | solution.py:275
  27.0 3.1 %collective-permute-start.2 = (bf16[8,256,128]{2,1,0:T(8,128)(2,1)S(1)}, bf16[8,256,128]{2,1,0:T(8,128)(2,1)S(1)}, u32[]{:S(2)}, u32[]{:S(2)}) collective-permute-start(bf16[8,256,128]{2,1,0:T(8,128)(2,1)S(1)} %all_to_all.10.refs_0_.own), channel_id=1, source_target_pairs={{48,0},{24,8},{0,16},{40,24},{16,32},{56,40},{32,48},{8,56},{112,6... | collective-permute-start | bytes 1572872 | tf_op jit(solution)/shard_map/ppermute | solution.py:266
  30.1 3.6 %collective-permute-start.1 = (bf16[8,256,128]{2,1,0:T(8,128)(2,1)S(1)}, bf16[8,256,128]{2,1,0:T(8,128)(2,1)S(1)}, u32[]{:S(2)}, u32[]{:S(2)}) collective-permute-start(bf16[8,256,128]{2,1,0:T(8,128)(2,1)S(1)} %all_to_all.10.refs_0_.own), channel_id=1, source_target_pairs={{64,0},{456,8},{80,16},{472,24},{96,32},{488,40},{112,48},{504,56}... | collective-permute-start | bytes 1572872 | tf_op jit(solution)/shard_map/ppermute | solution.py:266
  33.7 2.5 %collective-permute-start = (bf16[8,256,128]{2,1,0:T(8,128)(2,1)S(1)}, bf16[8,256,128]{2,1,0:T(8,128)(2,1)S(1)}, u32[]{:S(2)}, u32[]{:S(2)}) collective-permute-start(bf16[8,256,128]{2,1,0:T(8,128)(2,1)S(1)} %all_to_all.10.refs_0_.own), channel_id=1, source_target_pairs={{16,0},{56,8},{32,16},{8,24},{48,32},{24,40},{0,48},{40,56},{80,64... | collective-permute-start | bytes 1572872 | tf_op jit(solution)/shard_map/ppermute | solution.py:266
  36.2 1.0 %collective-permute-done.2.refs_3_ = bf16[8,256,128]{2,1,0:T(8,128)(2,1)S(1)} collective-permute-done((bf16[8,256,128]{2,1,0:T(8,128)(2,1)S(1)}, bf16[8,256,128]{2,1,0:T(8,128)(2,1)S(1)}, u32[]{:S(2)}, u32[]{:S(2)}) %collective-permute-start.2) | collective-permute-done | bytes 524320 | tf_op jit(solution)/shard_map/ppermute | solution.py:266
  37.2 4.3 %collective-permute-done.1.refs_2_ = bf16[8,256,128]{2,1,0:T(8,128)(2,1)S(1)} collective-permute-done((bf16[8,256,128]{2,1,0:T(8,128)(2,1)S(1)}, bf16[8,256,128]{2,1,0:T(8,128)(2,1)S(1)}, u32[]{:S(2)}, u32[]{:S(2)}) %collective-permute-start.1) | collective-permute-done | bytes 524320 | tf_op jit(solution)/shard_map/ppermute | solution.py:266
  41.5 5.2 %collective-permute-done.refs_1_ = bf16[8,256,128]{2,1,0:T(8,128)(2,1)S(1)} collective-permute-done((bf16[8,256,128]{2,1,0:T(8,128)(2,1)S(1)}, bf16[8,256,128]{2,1,0:T(8,128)(2,1)S(1)}, u32[]{:S(2)}, u32[]{:S(2)}) %collective-permute-start) | collective-permute-done | bytes 524320 | tf_op jit(solution)/shard_map/ppermute | solution.py:266
  46.8 0.1 pack.1.refs_0_
  46.9 1.9 %collective-permute-start.3 = (bf16[4,8,256,128]{3,2,1,0:T(8,128)(2,1)S(1)}, bf16[4,8,256,128]{3,2,1,0:T(8,128)(2,1)}, u32[]{:S(2)}, u32[]{:S(2)}) collective-permute-start(bf16[4,8,256,128]{3,2,1,0:T(8,128)(2,1)S(1)} %pack.1.refs_0_), channel_id=1, source_target_pairs={{8,0},{0,8},{24,16},{16,24},{40,32},{32,40},{56,48},{48,56},{72,64... | collective-permute-start | bytes 6291464 | tf_op jit(solution)/shard_map/ppermute | solution.py:266
  48.8 0.7 prepare.1
  49.5 12.0 %all-to-all-start.1 = ((bf16[64,8,128]{2,1,0:T(8,128)(2,1)}), bf16[64,8,128]{2,1,0:T(8,128)(2,1)S(1)}, u32[]{:S(2)}, u32[]{:S(2)}) async-start(bf16[64,8,128]{2,1,0:T(8,128)(2,1)} %prepare.1), calls=%async_computation.1 | async-start | bytes 262144 | tf_op jit(solution)/shard_map/all_to_all | solution.py:295
  61.5 0.6 copy.22
  62.1 0.6 copy.23
  62.7 0.6 copy.21
  63.3 0.0 collective-permute-done.3.refs_1_
  63.3 4.3 %decode.1 = (bf16[8,4,2,40,512]{4,3,2,1,0:T(8,128)(2,1)}, bf16[8,4,2,40,128]{4,3,2,1,0:T(8,128)(2,1)}, bf16[8,4,2,40,128]{4,3,2,1,0:T(8,128)(2,1)}, f32[1,512]{1...) custom-call(bf16[4,8,256,128]{3,2,1,0:T(8,128)(2,1)S(1)} %pack.1.refs_0_, ...), custom_call_target="tpu_custom_call" | custom-call | tf_op jit(solution)/shard_map/decode/pallas_call | solution.py:211
  67.6 2.9 %all-to-all-done.1 = bf16[64,8,128]{2,1,0:T(8,128)(2,1)S(1)} async-done(((bf16[64,8,128]{2,1,0:T(8,128)(2,1)}), bf16[64,8,128]{2,1,0:T(8,128)(2,1)S(1)}, u32[]{:S(2)}, u32[]{:S(2)}) %all-to-all-start.1) | async-done | bytes 131104 | tf_op jit(solution)/shard_map/all_to_all | solution.py:295
  70.5 0.8 %gather_norm.1 = bf16[20,128]{1,0:T(8,128)(2,1)} custom-call(bf16[4,2,8,8,128]{4,3,2,1,0:T(8,128)(2,1)S(1)} %bitcast.8, f32[1,512]{1,0:T(1,128)} %get-tuple-element.24._), custom_call_target="tpu_custom_call" | custom-call | tf_op jit(solution)/shard_map/gather_norm/pallas_call | solution.py:248
Async XLA Ops:
  27.0 10.2 %collective-permute-start.2 = (bf16[8,256,128]{2,1,0:T(8,128)(2,1)S(1)}, bf16[8,256,128]{2,1,0:T(8,128)(2,1)S(1)}, u32[]{:S(2)}, u32[]{:S(2)}) collective-permute-start(bf16[8,256,128]{2,1,0:T(8,128)(2,1)S(1)} %all_to_all.10.refs_0_.own), channel_id=1, source_target_pairs={{48,0},{24,8},{0,16},{40,24},{16,32},{56,40},{32,48},{8,56},{112,6... | collective-permute-start | bytes 1572872 | tf_op jit(solution)/shard_map/ppermute | solution.py:266
  30.1 11.4 %collective-permute-start.1 = (bf16[8,256,128]{2,1,0:T(8,128)(2,1)S(1)}, bf16[8,256,128]{2,1,0:T(8,128)(2,1)S(1)}, u32[]{:S(2)}, u32[]{:S(2)}) collective-permute-start(bf16[8,256,128]{2,1,0:T(8,128)(2,1)S(1)} %all_to_all.10.refs_0_.own), channel_id=1, source_target_pairs={{64,0},{456,8},{80,16},{472,24},{96,32},{488,40},{112,48},{504,56}... | collective-permute-start | bytes 1572872 | tf_op jit(solution)/shard_map/ppermute | solution.py:266
  33.7 13.1 %collective-permute-start = (bf16[8,256,128]{2,1,0:T(8,128)(2,1)S(1)}, bf16[8,256,128]{2,1,0:T(8,128)(2,1)S(1)}, u32[]{:S(2)}, u32[]{:S(2)}) collective-permute-start(bf16[8,256,128]{2,1,0:T(8,128)(2,1)S(1)} %all_to_all.10.refs_0_.own), channel_id=1, source_target_pairs={{16,0},{56,8},{32,16},{8,24},{48,32},{24,40},{0,48},{40,56},{80,64... | collective-permute-start | bytes 1572872 | tf_op jit(solution)/shard_map/ppermute | solution.py:266
  46.9 16.5 %collective-permute-start.3 = (bf16[4,8,256,128]{3,2,1,0:T(8,128)(2,1)S(1)}, bf16[4,8,256,128]{3,2,1,0:T(8,128)(2,1)}, u32[]{:S(2)}, u32[]{:S(2)}) collective-permute-start(bf16[4,8,256,128]{3,2,1,0:T(8,128)(2,1)S(1)} %pack.1.refs_0_), channel_id=1, source_target_pairs={{8,0},{0,8},{24,16},{16,24},{40,32},{32,40},{56,48},{48,56},{72,64... | collective-permute-start | bytes 6291464 | tf_op jit(solution)/shard_map/ppermute | solution.py:266
  49.5 21.0 %all-to-all-start.1 = ((bf16[64,8,128]{2,1,0:T(8,128)(2,1)}), bf16[64,8,128]{2,1,0:T(8,128)(2,1)S(1)}, u32[]{:S(2)}, u32[]{:S(2)}) async-start(bf16[64,8,128]{2,1,0:T(8,128)(2,1)} %prepare.1), calls=%async_computation.1 | async-start | bytes 262144 | tf_op jit(solution)/shard_map/all_to_all | solution.py:295

commit v3 on v2

--- a/solution.py
+++ b/solution.py
@@ -41,13 +41,16 @@
         pltpu.make_async_copy(s, d, sems.at[3 * n + i])
         for i, (s, d) in enumerate(zip(norms, (norm_train, norm_step)))
     ]
-    for load in loads + few_loads:
+    for at in sorted(range(n), key=lambda at: widths[at]):
+        for load in loads[3 * at : 3 * at + 3]:
+            load.start()
+    for load in few_loads:
         load.start()
     copies = wire.shape[0]
     rows = ins[0].shape[0]
     slabs = sum(w // LANES for w in widths)
-    slab = 0
-    for at, width in enumerate(widths):
+    for at in sorted(range(n), key=lambda at: widths[at]):
+        width, slab = widths[at], sum(w // LANES for w in widths[:at])
         train, drift, spread = ins[3 * at : 3 * at + 3]
         for load in loads[3 * at : 3 * at + 3]:
             load.wait()
@@ -275,7 +278,7 @@
     own = lax.all_to_all(wire, FSDP, 0, 0, axis_index_groups=same_kind, tiled=True)
     up = come_from(own, lambda y, x, c: (y, x + 1 - 2 * c, c))
     down = come_from(own, lambda y, x, c: (y, x - 1 + 2 * c, c))
-    side = come_from(own, lambda y, x, c: (y + 1 - 2 * c, x, c))
+    side = come_from(own, lambda y, x, c: (y - 1 + 2 * c, x, c))
     used = sum(w // LANES for w in widths) * rows + 7
     gain = prepare(used, NX * 2 * n_z, own)
     rest = []

time: 72.1 us -> 72.7 us (level)
  starting transfers between devices: 23.1 us -> 21.2 us
  waiting for transfers between devices: 13.5 us -> 15.4 us
    ppermute x4, starting transfers between devices: 11.1 us -> 9.21 us  [come_from(): lax.ppermute(value, FSDP, [(place(*source(*s)), place(*s)) for s in SPOTS])]
    ppermute x4, waiting for transfers between devices: 10.6 us -> 12.5 us  [come_from(): lax.ppermute(value, FSDP, [(place(*source(*s)), place(*s)) for s in SPOTS])]
where the time goes in v3:
time: 72.7 us; the launch traced here: 71.3 us
  blocking collectives  25 us (34%)
  starting transfers between devices  21.2 us (29%)
  waiting for transfers between devices  15.4 us (21%)
  Pallas kernels  7.2 us (10%)
  local copies, waits for them, and re-layouts  1.85 us (3%)
    all_to_all x1, blocking collectives, per_device(): lax.all_to_all(wire, FSDP, 0, 0, axis_index_groups=same_kind, tiled=True)  25 us
    ppermute x4, waiting for transfers between devices, come_from(): lax.ppermute(value, FSDP, [(place(*source(*s)), place(*s)) for s in SPOTS])  12.5 us
    all_to_all x1, starting transfers between devices, per_device(): lax.all_to_all(gain, FSDP + (Z,), 0, 0, axis_index_groups=rest, tiled=True)  12 us
    ppermute x4, starting transfers between devices, come_from(): lax.ppermute(value, FSDP, [(place(*source(*s)), place(*s)) for s in SPOTS])  9.21 us
    pallas_call x1, Pallas kernels, decode(): pl.pallas_call(functools.partial(decode_kernel, widths, rows), out_shape=...  4.29 us
    all_to_all x1, waiting for transfers between devices, per_device(): lax.all_to_all(gain, FSDP + (Z,), 0, 0, axis_index_groups=rest, tiled=True)  2.88 us
    unnamed x3, local copies, waits for them, and re-layouts  1.85 us
  transfers between devices with their start and end apart: 5, of which 4 were waited for; matrix products, arithmetic and copies ran while one was open for 3% of the time, Pallas kernels for 7%

profile of v3, /device:TPU:1, one launch (start us, length us, event | category | flops | bytes accessed | tf_op | source)
XLA Modules:
  0.0 71.3 jit_solution(8841937147964082406)
XLA Ops:
  0.6 1.3 %encode.1 = (f32[40,512]{1,0:T(8,128)S(1)}, f32[40,128]{1,0:T(8,128)S(1)}, f32[40,128]{1,0:T(8,128)S(1)}, bf16[8,256,128]{2,1,0:T(8,128)(2,1)S(1)}) custom-call(f32[5]{0:T(128)} %refs_0_.1, f32[5]{0:T(128)} %refs_1_.1, f32[40,512]{1,0:T(8,128)} %refs_2_.1, f32[40,512]{1,0:T(8,128)} %refs_3_.1, f32[40,512]{1,0:T(8,128)} %refs_4_.1, f32[40,128]{1,0:T(8,128)} %refs_5_.1, ...), custom_call_target="tpu_custom_call" | custom-call | tf_op jit(solution)/shard_map/encode/pallas_call | solution.py:101
  2.0 25.0 %all_to_all.10.refs_0_.own = bf16[8,256,128]{2,1,0:T(8,128)(2,1)S(1)} all-to-all(bf16[8,256,128]{2,1,0:T(8,128)(2,1)S(1)} %get-tuple-element.20), channel_id=1, replica_groups={{0,96,128,224,256,352,384,480},{16,112,144,240,272,368,400,496},{32,64,..., dimensions={0} | all-to-all | bytes 1048576 | tf_op jit(solution)/shard_map/all_to_all | solution.py:278
  26.9 3.1 %collective-permute-start.2 = (bf16[8,256,128]{2,1,0:T(8,128)(2,1)S(1)}, bf16[8,256,128]{2,1,0:T(8,128)(2,1)S(1)}, u32[]{:S(2)}, u32[]{:S(2)}) collective-permute-start(bf16[8,256,128]{2,1,0:T(8,128)(2,1)S(1)} %all_to_all.10.refs_0_.own), channel_id=1, source_target_pairs={{48,0},{24,8},{0,16},{40,24},{16,32},{56,40},{32,48},{8,56},{112,6... | collective-permute-start | bytes 1572872 | tf_op jit(solution)/shard_map/ppermute | solution.py:269
  30.1 2.3 %collective-permute-start.1 = (bf16[8,256,128]{2,1,0:T(8,128)(2,1)S(1)}, bf16[8,256,128]{2,1,0:T(8,128)(2,1)S(1)}, u32[]{:S(2)}, u32[]{:S(2)}) collective-permute-start(bf16[8,256,128]{2,1,0:T(8,128)(2,1)S(1)} %all_to_all.10.refs_0_.own), channel_id=1, source_target_pairs={{448,0},{72,8},{464,16},{88,24},{480,32},{104,40},{496,48},{120,56... | collective-permute-start | bytes 1572872 | tf_op jit(solution)/shard_map/ppermute | solution.py:269
  32.3 1.9 %collective-permute-start = (bf16[8,256,128]{2,1,0:T(8,128)(2,1)S(1)}, bf16[8,256,128]{2,1,0:T(8,128)(2,1)S(1)}, u32[]{:S(2)}, u32[]{:S(2)}) collective-permute-start(bf16[8,256,128]{2,1,0:T(8,128)(2,1)S(1)} %all_to_all.10.refs_0_.own), channel_id=1, source_target_pairs={{16,0},{56,8},{32,16},{8,24},{48,32},{24,40},{0,48},{40,56},{80,64... | collective-permute-start | bytes 1572872 | tf_op jit(solution)/shard_map/ppermute | solution.py:269
  34.3 2.9 %collective-permute-done.2.refs_3_ = bf16[8,256,128]{2,1,0:T(8,128)(2,1)S(1)} collective-permute-done((bf16[8,256,128]{2,1,0:T(8,128)(2,1)S(1)}, bf16[8,256,128]{2,1,0:T(8,128)(2,1)S(1)}, u32[]{:S(2)}, u32[]{:S(2)}) %collective-permute-start.2) | collective-permute-done | bytes 524320 | tf_op jit(solution)/shard_map/ppermute | solution.py:269
  37.1 3.4 %collective-permute-done.1.refs_2_ = bf16[8,256,128]{2,1,0:T(8,128)(2,1)S(1)} collective-permute-done((bf16[8,256,128]{2,1,0:T(8,128)(2,1)S(1)}, bf16[8,256,128]{2,1,0:T(8,128)(2,1)S(1)}, u32[]{:S(2)}, u32[]{:S(2)}) %collective-permute-start.1) | collective-permute-done | bytes 524320 | tf_op jit(solution)/shard_map/ppermute | solution.py:269
  40.5 6.2 %collective-permute-done.refs_1_ = bf16[8,256,128]{2,1,0:T(8,128)(2,1)S(1)} collective-permute-done((bf16[8,256,128]{2,1,0:T(8,128)(2,1)S(1)}, bf16[8,256,128]{2,1,0:T(8,128)(2,1)S(1)}, u32[]{:S(2)}, u32[]{:S(2)}) %collective-permute-start) | collective-permute-done | bytes 524320 | tf_op jit(solution)/shard_map/ppermute | solution.py:269
  46.7 0.1 pack.1.refs_0_
  46.9 1.9 %collective-permute-start.3 = (bf16[4,8,256,128]{3,2,1,0:T(8,128)(2,1)S(1)}, bf16[4,8,256,128]{3,2,1,0:T(8,128)(2,1)}, u32[]{:S(2)}, u32[]{:S(2)}) collective-permute-start(bf16[4,8,256,128]{3,2,1,0:T(8,128)(2,1)S(1)} %pack.1.refs_0_), channel_id=1, source_target_pairs={{8,0},{0,8},{24,16},{16,24},{40,32},{32,40},{56,48},{48,56},{72,64... | collective-permute-start | bytes 6291464 | tf_op jit(solution)/shard_map/ppermute | solution.py:269
  48.8 0.7 prepare.1
  49.5 12.0 %all-to-all-start.1 = ((bf16[64,8,128]{2,1,0:T(8,128)(2,1)}), bf16[64,8,128]{2,1,0:T(8,128)(2,1)S(1)}, u32[]{:S(2)}, u32[]{:S(2)}) async-start(bf16[64,8,128]{2,1,0:T(8,128)(2,1)} %prepare.1), calls=%async_computation.1 | async-start | bytes 262144 | tf_op jit(solution)/shard_map/all_to_all | solution.py:298
  61.5 0.6 copy.22
  62.1 0.6 copy.23
  62.7 0.6 copy.21
  63.3 0.0 collective-permute-done.3.refs_1_
  63.3 4.3 %decode.1 = (bf16[8,4,2,40,512]{4,3,2,1,0:T(8,128)(2,1)}, bf16[8,4,2,40,128]{4,3,2,1,0:T(8,128)(2,1)}, bf16[8,4,2,40,128]{4,3,2,1,0:T(8,128)(2,1)}, f32[1,512]{1...) custom-call(bf16[4,8,256,128]{3,2,1,0:T(8,128)(2,1)S(1)} %pack.1.refs_0_, ...), custom_call_target="tpu_custom_call" | custom-call | tf_op jit(solution)/shard_map/decode/pallas_call | solution.py:214
  67.6 2.9 %all-to-all-done.1 = bf16[64,8,128]{2,1,0:T(8,128)(2,1)S(1)} async-done(((bf16[64,8,128]{2,1,0:T(8,128)(2,1)}), bf16[64,8,128]{2,1,0:T(8,128)(2,1)S(1)}, u32[]{:S(2)}, u32[]{:S(2)}) %all-to-all-start.1) | async-done | bytes 131104 | tf_op jit(solution)/shard_map/all_to_all | solution.py:298
  70.5 0.8 %gather_norm.1 = bf16[20,128]{1,0:T(8,128)(2,1)} custom-call(bf16[4,2,8,8,128]{4,3,2,1,0:T(8,128)(2,1)S(1)} %bitcast.8, f32[1,512]{1,0:T(1,128)} %get-tuple-element.24._), custom_call_target="tpu_custom_call" | custom-call | tf_op jit(solution)/shard_map/gather_norm/pallas_call | solution.py:251
Async XLA Ops:
  26.9 10.2 %collective-permute-start.2 = (bf16[8,256,128]{2,1,0:T(8,128)(2,1)S(1)}, bf16[8,256,128]{2,1,0:T(8,128)(2,1)S(1)}, u32[]{:S(2)}, u32[]{:S(2)}) collective-permute-start(bf16[8,256,128]{2,1,0:T(8,128)(2,1)S(1)} %all_to_all.10.refs_0_.own), channel_id=1, source_target_pairs={{48,0},{24,8},{0,16},{40,24},{16,32},{56,40},{32,48},{8,56},{112,6... | collective-permute-start | bytes 1572872 | tf_op jit(solution)/shard_map/ppermute | solution.py:269
  30.1 10.5 %collective-permute-start.1 = (bf16[8,256,128]{2,1,0:T(8,128)(2,1)S(1)}, bf16[8,256,128]{2,1,0:T(8,128)(2,1)S(1)}, u32[]{:S(2)}, u32[]{:S(2)}) collective-permute-start(bf16[8,256,128]{2,1,0:T(8,128)(2,1)S(1)} %all_to_all.10.refs_0_.own), channel_id=1, source_target_pairs={{448,0},{72,8},{464,16},{88,24},{480,32},{104,40},{496,48},{120,56... | collective-permute-start | bytes 1572872 | tf_op jit(solution)/shard_map/ppermute | solution.py:269
  32.3 14.4 %collective-permute-start = (bf16[8,256,128]{2,1,0:T(8,128)(2,1)S(1)}, bf16[8,256,128]{2,1,0:T(8,128)(2,1)S(1)}, u32[]{:S(2)}, u32[]{:S(2)}) collective-permute-start(bf16[8,256,128]{2,1,0:T(8,128)(2,1)S(1)} %all_to_all.10.refs_0_.own), channel_id=1, source_target_pairs={{16,0},{56,8},{32,16},{8,24},{48,32},{24,40},{0,48},{40,56},{80,64... | collective-permute-start | bytes 1572872 | tf_op jit(solution)/shard_map/ppermute | solution.py:269
  46.9 16.5 %collective-permute-start.3 = (bf16[4,8,256,128]{3,2,1,0:T(8,128)(2,1)S(1)}, bf16[4,8,256,128]{3,2,1,0:T(8,128)(2,1)}, u32[]{:S(2)}, u32[]{:S(2)}) collective-permute-start(bf16[4,8,256,128]{3,2,1,0:T(8,128)(2,1)S(1)} %pack.1.refs_0_), channel_id=1, source_target_pairs={{8,0},{0,8},{24,16},{16,24},{40,32},{32,40},{56,48},{48,56},{72,64... | collective-permute-start | bytes 6291464 | tf_op jit(solution)/shard_map/ppermute | solution.py:269
  49.5 21.0 %all-to-all-start.1 = ((bf16[64,8,128]{2,1,0:T(8,128)(2,1)}), bf16[64,8,128]{2,1,0:T(8,128)(2,1)S(1)}, u32[]{:S(2)}, u32[]{:S(2)}) async-start(bf16[64,8,128]{2,1,0:T(8,128)(2,1)} %prepare.1), calls=%async_computation.1 | async-start | bytes 262144 | tf_op jit(solution)/shard_map/all_to_all | solution.py:298
